TPU v7x, 32 devices: a whole 2x2x4 slice. The times are simulated.
32 devices in a mesh: flow: 8 (over z, x), leaf: 4 (over y, core).
Axes of the slice: x: 2, y: 2, z: 4, core: 2. Of those that a mesh axis runs over, the one named last changes fastest.
Arguments:
- vel_coef: float32 [81, 16384], P(None, 'flow'), may hold values from -6 to 6
- gp_block: int32 [65536, 1], P(('flow', 'leaf')), may hold values from 0 to 7; in each aligned block of 2048 rows (0 to 2047, 2048 to 4095, ...) at most 512 rows name the same one
- gp_elem: int32 [65536], P(('flow', 'leaf')), may hold values from 0 to 2047
- gp_param: float32 [3, 65536], P(None, ('flow', 'leaf')), may hold values from 0 to 1
- gp_vel: float32 [3, 65536], P(None, ('flow', 'leaf')), may hold values from -6 to 6
- gp_weight: float32 [65536], P(('flow', 'leaf')), may hold values from 0.1 to 1
- gp_pos: float32 [3, 65536], P(None, ('flow', 'leaf')), may hold values from -4 to 4
- contact_patch: int32 [65536], P(('flow', 'leaf')), may hold values from 0 to 1023
- contact_param: float32 [2, 65536], P(None, ('flow', 'leaf')), may hold values from 0 to 1
- patch_ctrl: float32 [27, 8192], P(None, ('flow', 'leaf')), may hold values from -4 to 4
Outputs:
- flow_force: float32 [81, 16384], P(None, ('flow', 'leaf'))
- shell_force: float32 [3, 65536], P(None, ('flow', 'leaf'))
- patch_force: float32 [27, 8192], P(None, ('flow', 'leaf'))
Inputs may be any that keep to these rules, and one draw needn't show every extreme that they name: `gp_block`: the Gauss points of one device lie in at most 512 of each flow block's elements; some block is reached with exactly 512. `contact_patch`: A contact partner is one of the 1024 patches held by the Gauss point's own group, the devices of one index of flow.
All inputs are finite; a program needn't handle non-finite values.
Results may differ from a plain program's by a relative error of at most 0.0001.
Values sent between devices are 32-bit elements; how exact they have to be, the bound alone decides.
No kernel may reach another device: no remote copies, remote signals or barrier semaphores. Data moves between devices by JAX's collectives and lax.ppermute only.
A program may use at most 64 MiB of HBM per device.

v0:
```python
import jax
import jax.numpy as jnp
from jax import lax
from jax.sharding import PartitionSpec as P

BETA = 1.5
STIFF = 2.0
REACH = 0.5


def basis(x):
    return jnp.stack([0.5 * (1.0 - x) ** 2, 0.5 * (1.0 + 2.0 * x - 2.0 * x * x), 0.5 * x * x])


def solid_weights(param):
    first, second, third = (basis(param[0]), basis(param[1]), basis(param[2]))
    return (first[:, None, None, :] * second[None, :, None, :] * third[None, None, :, :]).reshape(
        27, -1
    )


def shell_weights(param):
    first, second = (basis(param[0]), basis(param[1]))
    return (first[:, None, :] * second[None, :, :]).reshape(9, -1)


def contact_force(position, partner_coef, weights):
    near = jnp.sum(partner_coef.reshape(3, 9, -1) * weights[None], axis=1)
    gap = position - near
    return STIFF * gap / (1.0 + jnp.sum(gap * gap, axis=0) / (REACH * REACH))


def decode(block, limit):
    flat = block.reshape(block.shape[0], -1)
    valid = flat[0] >= 0.0
    index = jnp.clip(flat[0].astype(jnp.int32), 0, limit - 1)
    return (flat, valid, index)


def take_columns(source, index):
    return jnp.transpose(jnp.transpose(source)[index])


def add_columns(columns, index, values):
    return jnp.transpose(
        jnp.zeros((columns, values.shape[0]), jnp.float32).at[index].add(jnp.transpose(values))
    )


def sample_flow(coef, index, weights):
    picked = take_columns(coef, index).reshape(3, 27, -1)
    return jnp.sum(picked * weights[None], axis=1)


def spread_rows(columns, index, weights, force):
    terms = (force[:, None, :] * weights[None]).reshape(81, -1)
    return add_columns(columns, index, terms)


def per_device(
    vel_coef,
    gp_block,
    gp_elem,
    gp_param,
    gp_vel,
    gp_weight,
    gp_pos,
    contact_patch,
    contact_param,
    patch_ctrl,
):
    owners = lax.axis_size("flow")
    peers = lax.axis_size("leaf")
    count = gp_elem.shape[0]
    slots_per = 2 * count // owners
    width = slots_per * owners
    elements = vel_coef.shape[1]
    dest = gp_block[:, 0]
    order = jnp.argsort(dest, stable=True)
    sorted_dest = dest[order]
    tally = jnp.sum(
        (dest[:, None] == jnp.arange(owners, dtype=jnp.int32)[None, :]).astype(jnp.int32), axis=0
    )
    starts = jnp.cumsum(tally) - tally
    rank_sorted = jnp.arange(count, dtype=jnp.int32) - starts[sorted_dest]
    slot = jnp.zeros((count,), jnp.int32).at[order].set(rank_sorted * owners + sorted_dest)

    def pack(values, filler):
        buffer = (
            jnp.full((width, values.shape[0]), filler, jnp.float32)
            .at[slot]
            .set(jnp.transpose(values))
        )
        return jnp.transpose(buffer).reshape(values.shape[0], slots_per, owners)

    elem_row = gp_elem.astype(jnp.float32)[None, :]
    payload = pack(jnp.concatenate([elem_row, gp_param, gp_vel, gp_weight[None, :]], axis=0), 0.0)
    occupied = pack(jnp.ones((1, count), jnp.float32), 0.0)
    payload = jnp.concatenate(
        [payload[:1] - (occupied < 0.5).astype(jnp.float32), payload[1:]], axis=0
    )
    block = lax.all_to_all(payload, "flow", split_axis=2, concat_axis=2, tiled=True)
    flat, valid, index = decode(block, elements)
    speed = sample_flow(vel_coef, index, solid_weights(flat[1:4]))
    force = BETA * flat[7][None, :] * (flat[4:7] - speed) * valid[None, :].astype(jnp.float32)
    force = force.reshape(3, block.shape[1], block.shape[2])
    back = lax.all_to_all(force, "flow", split_axis=2, concat_axis=2, tiled=True)
    result = (back, force, block)
    back, arrived, kept = result
    fsi = take_columns(back.reshape(3, width), slot)
    flat, valid, index = decode(kept, elements)
    force = arrived.reshape(3, width) * valid[None, :].astype(jnp.float32)
    piece = lax.all_gather(patch_ctrl, "leaf", axis=1, tiled=True)
    inside = (contact_patch >= 0) & (contact_patch < piece.shape[1])
    taken = take_columns(piece, jnp.clip(contact_patch, 0, piece.shape[1] - 1))
    partner_coef = jnp.where(inside[None, :], taken, jnp.zeros((27, count), jnp.float32))
    shell_w = shell_weights(contact_param)
    pushes = contact_force(gp_pos, partner_coef, shell_w)
    reaction = -(pushes[:, None, :] * shell_w[None]).reshape(27, -1)
    patch_term = add_columns(patch_ctrl.shape[1] * peers, contact_patch, reaction)
    partial_value = spread_rows(elements, index, solid_weights(flat[1:4]), force)
    flow_force, patch_force = (
        lax.psum_scatter(partial_value, "leaf", scatter_dimension=1, tiled=True),
        lax.psum_scatter(patch_term, "leaf", scatter_dimension=1, tiled=True),
    )
    shell_force = pushes - fsi
    return (flow_force, shell_force, patch_force)


def solution(mesh):
    in_specs = (
        P(None, "flow"),
        P(("flow", "leaf"), None),
        P(("flow", "leaf")),
        P(None, ("flow", "leaf")),
        P(None, ("flow", "leaf")),
        P(("flow", "leaf")),
        P(None, ("flow", "leaf")),
        P(("flow", "leaf")),
        P(None, ("flow", "leaf")),
        P(None, ("flow", "leaf")),
    )
    out_specs = (P(None, ("flow", "leaf")), P(None, ("flow", "leaf")), P(None, ("flow", "leaf")))
    return jax.shard_map(
        per_device, mesh=mesh, in_specs=in_specs, out_specs=out_specs, check_vma=False
    )
```

profile of v0, /device:TPU:0, one launch (start us, length us, event | category | flops | bytes accessed | tf_op | source)
XLA Modules:
  0.0 198.3 jit_solution(7097408671395012003)
XLA Ops:
  7.2 0.9 convert_reduce_fusion
  8.1 0.2 reduce-window.9
  8.3 0.7 fusion.28
  9.0 5.7 %sort.17 = (s32[2048]{0:T(1024)}, s32[2048]{0:T(1024)S(1)}) sort(s32[2048]{0:T(1024)} %bitcast.41, s32[2048]{0:T(1024)S(1)} %iota.11), dimensions={0}, to_apply=%region_0.0 | sort | flops 22528 | bytes 32768 | tf_op jit(solution)/shard_map/jit(argsort)/sort | solution.py:79
  14.8 11.8 %gather_fusion = s32[2048]{0:T(1024)S(1)} fusion(s32[2048]{0:T(1024)S(1)} %bitcast.42, s32[2048]{0:T(1024)S(1)} %get-tuple-element.53), kind=kCustom, calls=%fused_computation | custom fusion | bytes 24576 | tf_op jit(solution)/shard_map/gather | solution.py:80
  26.6 4.4 %compare_select_fusion.2 = s32[2048,1]{0,1:T(1,128)S(1)} fusion(s32[]{:T(128)} %bitcast.5, s32[]{:T(128)} %bitcast.6, s32[]{:T(128)} %bitcast.7, s32[]{:T(128)} %bitcast.8, s32[]{:T(128)} %bitcast.9, s32[]{:T(128)} %bitcast.11, s32[]{:T(128)} %bitcast.10, s32[2048,1]{0,1:T(1,128)S(1)} %bitcast.54), kind=kLoop, calls=%fused_computation.44 | loop fusion | flops 30720 | bytes 16412 | tf_op jit(solution)/shard_map/gather | solution.py:85
  31.0 0.7 fusion.22
  31.7 8.0 %scatter_custom_fusion = s32[2048]{0:T(1024)S(1)} fusion(s32[2048]{0:T(1024)S(1)} %get-tuple-element.54, s32[2048]{0:T(1024)S(1)} %fusion.22, s32[]{:T(128)} %constant.14.clone.1), kind=kCustom, calls=%fused_computation.99 | custom fusion | bytes 8196 | tf_op jit(solution)/shard_map/scatter | solution.py:86
  39.7 0.6 broadcast_clamp_fusion.1
  40.4 0.3 copy.139
  40.7 6.1 %scatter_custom_fusion.1 = f32[4096,8]{1,0:T(8,128)S(1)} fusion(s32[2048]{0:T(1024)S(1)} %get-tuple-element.52, f32[2048,8]{1,0:T(8,128)S(1)} %copy.139, f32[]{:T(128)} %constant.13.clone.1), kind=kCustom, calls=%fused_computation.13 | custom fusion | bytes 131076 | tf_op jit(solution)/shard_map/scatter | solution.py:92
  46.8 0.6 slice_reduce_fusion
  47.5 2.0 slice_bitcast_fusion
  49.6 8.1 %scatter_custom_fusion.2 = f32[4096]{0:T(1024)S(1)} fusion(s32[2048]{0:T(1024)S(1)} %get-tuple-element.52, f32[2048]{0:T(1024)S(1)} %broadcast.365, f32[]{:T(128)} %constant.13.clone.1), kind=kCustom, calls=%fused_computation.88 | custom fusion | bytes 16388 | tf_op jit(solution)/shard_map/scatter | solution.py:92
  58.0 2.2 %copy.141 = f32[7,512,8]{1,0,2:T(8,128)S(1)} copy(f32[7,512,8]{0,2,1:T(8,128)} %slice_bitcast_fusion) | data formatting | bytes 229376 | tf_op jit(solution)/shard_map/slice | solution.py:100
  60.2 0.7 pad_maximum_fusion
  60.9 7.3 %all-to-all-start = ((f32[8,512,8]{1,0,2:T(8,128)}), f32[8,512,8]{1,0,2:T(8,128)S(1)}, u32[]{:S(2)}, u32[]{:S(2)}) async-start(f32[8,512,8]{1,0,2:T(8,128)} %pad_maximum_fusion), calls=%async_computation | async-start | bytes 262144 | tf_op jit(solution)/shard_map/all_to_all | solution.py:102
  68.2 0.6 compare_select_fusion.8
  69.1 7.4 %all_gather.3 = f32[27,1024]{0,1:T(8,128)S(1)} all-gather(f32[27,256]{0,1:T(8,128)S(1)} %copy.155), channel_id=1, replica_groups=mesh['flow'=8,'leaf'=4] {'leaf'}, dimensions={1}, use_global_device_ids=true | all-gather | bytes 138240 | tf_op jit(solution)/shard_map/all_gather | solution.py:113
  76.5 5.5 %gather_fusion.2 = f32[2048,27]{1,0:T(8,128)S(1)} fusion(f32[1024,27]{1,0:T(8,128)S(1)} %bitcast.44, s32[2048]{0:T(1024)S(1)} %get-tuple-element.50), kind=kCustom, calls=%fused_computation.2 | custom fusion | bytes 450560 | tf_op jit(solution)/shard_map/gather | solution.py:41
  82.0 0.3 select_bitcast_fusion
  82.4 0.3 copy.156
  82.9 0.2 copy-done.2
  83.1 0.3 copy.148
  83.5 0.6 multiply_add_fusion.5
  85.6 1.0 mul.473
  87.0 10.8 %gather_fusion.1 = f32[4096,81]{1,0:T(8,128)S(1)} fusion(f32[2048,81]{1,0:T(8,128)S(1)} %bitcast.43, s32[4096]{0:T(1024)S(1)} %broadcast_clamp_fusion), kind=kCustom, calls=%fused_computation.1 | custom fusion | bytes 2670592 | tf_op jit(solution)/shard_map/gather | solution.py:41
  97.8 1.8 copy.149
  99.5 1.6 reshape.456
  101.1 0.2 multiply_reduce_fusion
  101.4 0.4 reduce_sum.42
  101.8 0.2 copy.157
  102.1 0.3 copy.147
  102.4 0.7 copy.158
  103.1 6.0 %all-to-all-start.1 = ((f32[3,512,8]{1,0,2:T(4,128)}), f32[3,512,8]{1,0,2:T(4,128)S(1)}, u32[]{:S(2)}, u32[]{:S(2)}) async-start(f32[3,512,8]{1,0,2:T(4,128)} %copy.158), calls=%async_computation.2 | async-start | bytes 131072 | tf_op jit(solution)/shard_map/all_to_all | solution.py:107
  109.1 0.4 slice.63
  110.2 5.8 %all-to-all-done.1 = f32[3,512,8]{1,0,2:T(4,128)S(1)} async-done(((f32[3,512,8]{1,0,2:T(4,128)}), f32[3,512,8]{1,0,2:T(4,128)S(1)}, u32[]{:S(2)}, u32[]{:S(2)}) %all-to-all-start.1) | async-done | bytes 49184 | tf_op jit(solution)/shard_map/all_to_all | solution.py:107
  116.0 0.8 copy.159
  116.8 7.6 %gather_fusion.3 = f32[2048,3]{1,0:T(8,128)} fusion(f32[4096,3]{1,0:T(8,128)S(1)} %bitcast.45, s32[2048]{0:T(1024)S(1)} %copy-done.9), kind=kCustom, calls=%fused_computation.3 | custom fusion | bytes 57344 | tf_op jit(solution)/shard_map/gather | solution.py:41
  124.4 1.6 copy.160
  125.9 0.6 bitcast_subtract_fusion
  126.7 0.4 copy.161
  127.0 12.4 %scatter_custom_fusion.4 = f32[1024,27]{1,0:T(8,128)} fusion(s32[2048]{0:T(1024)} %get-tuple-element.49, f32[2048,27]{1,0:T(8,128)S(1)} %copy.161, f32[]{:T(128)} %constant.13.clone.1), kind=kCustom, calls=%fused_computation.21 | custom fusion | flops 55296 | bytes 111104 | tf_op jit(solution)/shard_map/scatter-add | solution.py:46
  139.8 0.8 copy.154
  140.7 23.4 %scatter_custom_fusion.3 = f32[2048,81]{1,0:T(8,128)} fusion(s32[4096]{0:T(1024)S(1)} %bitcast.56, f32[4096,81]{1,0:T(8,128)S(1)} %copy.154, f32[]{:T(128)} %constant.13.clone.1), kind=kCustom, calls=%fused_computation.16 | custom fusion | flops 331776 | bytes 663556 | tf_op jit(solution)/shard_map/scatter-add | solution.py:46
  164.1 1.6 copy.163
  165.7 24.0 %reduce-scatter.3.cloned.1.call-done = f32[81,512]{0,1:T(8,128)} async-done(((f32[81,2048]{0,1:T(8,128)}), f32[81,512]{0,1:T(8,128)}) %reduce-scatter.3.cloned.1.call-update) | async-done | bytes 165904 | tf_op jit(solution)/shard_map/reduce_scatter | solution.py:123
  189.7 1.8 copy.162
  (84 shorter events, 3.9 us)
Async XLA Ops:
  7.2 7.5 %copy-start = (s32[2048,1]{0,1:T(1,128)S(1)}, s32[2048,1]{0,1:T(1,128)}, u32[]{:S(2)}) copy-start(s32[2048,1]{0,1:T(1,128)} %param.11) | copy-start | bytes 24580
  14.7 25.6 %copy-start.12 = (s32[2048]{0:T(1024)S(1)}, s32[2048]{0:T(1024)}, u32[]{:S(2)}) copy-start(s32[2048]{0:T(1024)} %param.12) | copy-start | bytes 24580
  14.7 25.6 %copy-start.6 = (f32[3,2048]{1,0:T(4,128)S(1)}, f32[3,2048]{1,0:T(4,128)}, u32[]{:S(2)}) copy-start(f32[3,2048]{1,0:T(4,128)} %param.14) | copy-start | bytes 73732
  14.7 25.6 %copy-start.7 = (f32[3,2048]{1,0:T(4,128)S(1)}, f32[3,2048]{1,0:T(4,128)}, u32[]{:S(2)}) copy-start(f32[3,2048]{1,0:T(4,128)} %param.13) | copy-start | bytes 73732
  14.7 25.6 %copy-start.11 = (f32[2048]{0:T(1024)S(1)}, f32[2048]{0:T(1024)}, u32[]{:S(2)}) copy-start(f32[2048]{0:T(1024)} %param.15) | copy-start | bytes 24580
  49.6 18.6 %copy-start.5 = (s32[2048]{0:T(1024)S(1)}, s32[2048]{0:T(1024)}, u32[]{:S(2)}) copy-start(s32[2048]{0:T(1024)} %param.17) | copy-start | bytes 24580
  49.6 19.2 %copy-start.10 = (f32[2,2048]{1,0:T(2,128)S(1)}, f32[2,2048]{1,0:T(2,128)}, u32[]{:S(2)}) copy-start(f32[2,2048]{1,0:T(2,128)} %param.18) | copy-start | bytes 49156
  57.9 11.2 %copy-start.4 = (f32[27,256]{1,0:T(8,128)S(1)}, f32[27,256]{1,0:T(8,128)}, u32[]{:S(2)}) copy-start(f32[27,256]{1,0:T(8,128)} %param.19) | copy-start | bytes 82948
  60.9 23.1 %all-to-all-start = ((f32[8,512,8]{1,0,2:T(8,128)}), f32[8,512,8]{1,0,2:T(8,128)S(1)}, u32[]{:S(2)}, u32[]{:S(2)}) async-start(f32[8,512,8]{1,0,2:T(8,128)} %pad_maximum_fusion), calls=%async_computation | async-start | bytes 262144 | tf_op jit(solution)/shard_map/all_to_all | solution.py:102
  82.0 0.8 copy-start.3
  82.0 1.1 copy-start.2
  99.5 1.6 copy-start.1
  103.1 12.9 %all-to-all-start.1 = ((f32[3,512,8]{1,0,2:T(4,128)}), f32[3,512,8]{1,0,2:T(4,128)S(1)}, u32[]{:S(2)}, u32[]{:S(2)}) async-start(f32[3,512,8]{1,0,2:T(4,128)} %copy.158), calls=%async_computation.2 | async-start | bytes 131072 | tf_op jit(solution)/shard_map/all_to_all | solution.py:107
  109.1 7.7 %copy-start.9 = (s32[2048]{0:T(1024)S(1)}, s32[2048]{0:T(1024)}, u32[]{:S(2)}) copy-start(s32[2048]{0:T(1024)} %get-tuple-element.51) | copy-start | bytes 24580
  109.1 55.0 %reduce-scatter.5.cloned.1.call-start = ((), (), s32[]{:S(2)}) async-start(), calls=%async_computation.5 | async-start | bytes 655360 | tf_op jit(solution)/shard_map/reduce_scatter | solution.py:124
  116.8 9.1 %copy-start.8 = (f32[2048]{0:T(1024)S(1)}, f32[2048]{0:T(1024)}, u32[]{:S(2)}) copy-start(f32[2048]{0:T(1024)} %multiply_add_fusion.5) | copy-start | bytes 24580
  139.4 50.2 %reduce-scatter.3.cloned.1.call-start = ((), (), s32[]{:S(2)}) async-start(), calls=%async_computation.4 | async-start | bytes 1310720 | tf_op jit(solution)/shard_map/reduce_scatter | solution.py:123
Sparse Core Ops, SparseCore 0:
  139.6 18.4 reduce-scatter.4
  164.2 25.4 reduce-scatter.2
where the time goes:
time: 199 us; the launch traced here: 198 us
  local copies, waits for them, and re-layouts  80.6 us (41%)
  other arithmetic  52.5 us (26%)
  waiting for transfers between devices  29.9 us (15%)
  between operations  14.7 us (7%)
  starting transfers between devices  13.4 us (7%)
  blocking collectives  7.37 us (4%)
    scatter-add x2, other arithmetic, add_columns(): jnp.zeros((columns, values.shape[0]), jnp.float32).at[index]  35.7 us
    gather x4, local copies, waits for them, and re-layouts, take_columns(): return jnp.transpose(jnp.transpose(source)[index])  25.4 us
    reduce_scatter x1, waiting for transfers between devices, per_device(): lax.psum_scatter(partial_value, 'leaf', scatter_dimension=1, tiled=True)  24 us
    scatter x2, local copies, waits for them, and re-layouts, pack(): buffer = jnp.full((width, values.shape[0]), filler, jnp.float32).at[slot]...  14.2 us
    gather x1, local copies, waits for them, and re-layouts, per_device(): sorted_dest = dest[order]  11.8 us
    scatter x1, local copies, waits for them, and re-layouts, per_device(): jnp.zeros((count,), jnp.int32).at[order]  8.05 us
    all_gather x1, blocking collectives, per_device(): piece = lax.all_gather(patch_ctrl, 'leaf', axis=1, tiled=True)  7.37 us
    all_to_all x1, starting transfers between devices, per_device(): lax.all_to_all(payload, 'flow', split_axis=2, concat_axis=2, tiled=True)  7.28 us
  transfers between devices with their start and end apart: 4, of which 2 were waited for; matrix products, arithmetic and copies ran while one was open for 18% of the time, Pallas kernels for 0%

commit v1 on v0

--- a/solution.py
+++ b/solution.py
@@ -104,7 +104,18 @@
     speed = sample_flow(vel_coef, index, solid_weights(flat[1:4]))
     force = BETA * flat[7][None, :] * (flat[4:7] - speed) * valid[None, :].astype(jnp.float32)
     force = force.reshape(3, block.shape[1], block.shape[2])
-    back = lax.all_to_all(force, "flow", split_axis=2, concat_axis=2, tiled=True)
+    ways, here = (lax.axis_size("flow"), lax.axis_index("flow"))
+    width_2 = force.shape[2] // ways
+    dims = list(force.shape)
+    dims[2] = width_2
+    height = dims[2]
+    dims[2] = height * ways
+    back = jnp.zeros(dims, force.dtype)
+    for mask in range(ways):
+        part = lax.dynamic_slice_in_dim(force, (here ^ mask) * width_2, width_2, axis=2)
+        if mask:
+            part = lax.ppermute(part, "flow", [(d, d ^ mask) for d in range(ways)])
+        back = lax.dynamic_update_slice_in_dim(back, part, (here ^ mask) * height, axis=2)
     result = (back, force, block)
     back, arrived, kept = result
     fsi = take_columns(back.reshape(3, width), slot)

time: 199 us -> 273 us (1.37)
  local copies, waits for them, and re-layouts: 80.6 us -> 149 us
  starting transfers between devices: 13.4 us -> 19.1 us
  waiting for transfers between devices: 29.9 us -> 26.2 us
    dynamic_update_slice x0 -> x8, local copies, waits for them, and re-layouts: none -> 47.3 us  [per_device(): lax.dynamic_update_slice_in_dim(back, part, (here ^ mask) * height, axis=2)]
    dynamic_slice x0 -> x9, local copies, waits for them, and re-layouts: none -> 13.3 us  [per_device(): lax.dynamic_slice_in_dim(force, (here ^ mask) * width_2, width_2, axis=2)]
    ppermute x0 -> x7, starting transfers between devices: none -> 11.7 us  [per_device(): part = lax.ppermute(part, 'flow', [(d, d ^ mask) for d in range(ways)])]
    all_to_all x1 -> x0, starting transfers between devices: 5.99 us -> none  [per_device(): lax.all_to_all(force, 'flow', split_axis=2, concat_axis=2, tiled=True)]
    all_to_all x1 -> x0, waiting for transfers between devices: 5.81 us -> none  [per_device(): lax.all_to_all(force, 'flow', split_axis=2, concat_axis=2, tiled=True)]
    ppermute x0 -> x7, local copies, waits for them, and re-layouts: none -> 4.44 us  [per_device(): part = lax.ppermute(part, 'flow', [(d, d ^ mask) for d in range(ways)])]
    unnamed x30 -> x57, local copies, waits for them, and re-layouts: 4.14 us -> 6.09 us
  transfers between devices with their start and end apart: 4 -> 10, of which waited for: 2 -> 1; matrix products, arithmetic and copies ran while one was open for 18% -> 32% of each run, Pallas kernels for 0% -> 0%
where the time goes in v1:
time: 273 us; the launch traced here: 272 us
  local copies, waits for them, and re-layouts  149 us (55%)
  other arithmetic  55.1 us (20%)
  waiting for transfers between devices  26.2 us (10%)
  starting transfers between devices  19.1 us (7%)
  between operations  15 us (5%)
  blocking collectives  7.19 us (3%)
    dynamic_update_slice x8, local copies, waits for them, and re-layouts, per_device(): lax.dynamic_update_slice_in_dim(back, part, (here ^ mask) * height, axis=2)  47.3 us
    scatter-add x2, other arithmetic, add_columns(): jnp.zeros((columns, values.shape[0]), jnp.float32).at[index]  35.8 us
    gather x4, local copies, waits for them, and re-layouts, take_columns(): return jnp.transpose(jnp.transpose(source)[index])  27.3 us
    reduce_scatter x1, waiting for transfers between devices, per_device(): lax.psum_scatter(partial_value, 'leaf', scatter_dimension=1, tiled=True)  26.1 us
    scatter x2, local copies, waits for them, and re-layouts, pack(): buffer = jnp.full((width, values.shape[0]), filler, jnp.float32).at[slot]...  14.2 us
    dynamic_slice x9, local copies, waits for them, and re-layouts, per_device(): lax.dynamic_slice_in_dim(force, (here ^ mask) * width_2, width_2, axis=2)  13.3 us
    gather x1, local copies, waits for them, and re-layouts, per_device(): sorted_dest = dest[order]  11.8 us
    ppermute x7, starting transfers between devices, per_device(): part = lax.ppermute(part, 'flow', [(d, d ^ mask) for d in range(ways)])  11.7 us
  transfers between devices with their start and end apart: 10, of which 1 were waited for; matrix products, arithmetic and copies ran while one was open for 32% of the time, Pallas kernels for 0%

profile of v1, /device:TPU:0, one launch (start us, length us, event | category | flops | bytes accessed | tf_op | source)
XLA Modules:
  0.0 272.0 jit_solution(68092845069776136)
XLA Ops:
  7.2 0.9 convert_reduce_fusion
  9.6 5.7 %sort.17 = (s32[2048]{0:T(1024)}, s32[2048]{0:T(1024)S(1)}) sort(s32[2048]{0:T(1024)} %bitcast.44, s32[2048]{0:T(1024)S(1)} %iota.11), dimensions={0}, to_apply=%region_0.0 | sort | flops 22528 | bytes 32768 | tf_op jit(solution)/shard_map/jit(argsort)/sort | solution.py:79
  15.4 11.8 %gather_fusion = s32[2048]{0:T(1024)S(1)} fusion(s32[2048]{0:T(1024)S(1)} %bitcast.45, s32[2048]{0:T(1024)S(1)} %get-tuple-element.64), kind=kCustom, calls=%fused_computation | custom fusion | bytes 24576 | tf_op jit(solution)/shard_map/gather | solution.py:80
  27.3 4.4 %compare_select_fusion.2 = s32[2048,1]{0,1:T(1,128)S(1)} fusion(s32[]{:T(128)} %bitcast.5, s32[]{:T(128)} %bitcast.6, s32[]{:T(128)} %bitcast.7, s32[]{:T(128)} %bitcast.8, s32[]{:T(128)} %bitcast.9, s32[]{:T(128)} %bitcast.11, s32[]{:T(128)} %bitcast.10, s32[2048,1]{0,1:T(1,128)S(1)} %bitcast.57), kind=kLoop, calls=%fused_computation.42 | loop fusion | flops 30720 | bytes 16412 | tf_op jit(solution)/shard_map/gather | solution.py:85
  32.3 8.0 %scatter_custom_fusion = s32[2048]{0:T(1024)S(1)} fusion(s32[2048]{0:T(1024)S(1)} %get-tuple-element.65, s32[2048]{0:T(1024)S(1)} %fusion.20, s32[]{:T(128)} %constant.23.clone.1), kind=kCustom, calls=%fused_computation.97 | custom fusion | bytes 8196 | tf_op jit(solution)/shard_map/scatter | solution.py:86
  41.3 6.1 %scatter_custom_fusion.1 = f32[4096,8]{1,0:T(8,128)S(1)} fusion(s32[2048]{0:T(1024)S(1)} %get-tuple-element.63, f32[2048,8]{1,0:T(8,128)S(1)} %copy.211, f32[]{:T(128)} %constant.22.clone.1), kind=kCustom, calls=%fused_computation.13 | custom fusion | bytes 131076 | tf_op jit(solution)/shard_map/scatter | solution.py:92
  48.1 2.0 slice_bitcast_fusion
  50.0 8.1 %scatter_custom_fusion.2 = f32[4096]{0:T(1024)S(1)} fusion(s32[2048]{0:T(1024)S(1)} %get-tuple-element.63, f32[2048]{0:T(1024)S(1)} %broadcast.365, f32[]{:T(128)} %constant.22.clone.1), kind=kCustom, calls=%fused_computation.86 | custom fusion | bytes 16388 | tf_op jit(solution)/shard_map/scatter | solution.py:92
  58.3 2.2 copy.213
  61.5 7.3 %all-to-all-start = ((f32[8,512,8]{1,0,2:T(8,128)}), f32[8,512,8]{1,0,2:T(8,128)S(1)}, u32[]{:S(2)}, u32[]{:S(2)}) async-start(f32[8,512,8]{1,0,2:T(8,128)} %pad_maximum_fusion), calls=%async_computation | async-start | bytes 262144 | tf_op jit(solution)/shard_map/all_to_all | solution.py:102
  69.8 7.2 %all_gather.3 = f32[27,1024]{0,1:T(8,128)S(1)} all-gather(f32[27,256]{0,1:T(8,128)S(1)} %copy.226), channel_id=1, replica_groups=mesh['flow'=8,'leaf'=4] {'leaf'}, dimensions={1}, use_global_device_ids=true | all-gather | bytes 138240 | tf_op jit(solution)/shard_map/all_gather | solution.py:124
  77.0 5.5 %gather_fusion.2 = f32[2048,27]{1,0:T(8,128)S(1)} fusion(f32[1024,27]{1,0:T(8,128)S(1)} %bitcast.47, s32[2048]{0:T(1024)S(1)} %get-tuple-element.61), kind=kCustom, calls=%fused_computation.2 | custom fusion | bytes 450560 | tf_op jit(solution)/shard_map/gather | solution.py:41
  85.6 0.9 copy.229
  88.9 1.0 mul.473
  89.9 1.2 copy.251
  91.1 12.7 %gather_fusion.1 = f32[4096,81]{1,0:T(8,128)S(1)} fusion(f32[2048,81]{1,0:T(8,128)S(1)} %bitcast.46, s32[4096]{0:T(1024)} %broadcast_clamp_fusion), kind=kCustom, calls=%fused_computation.1 | custom fusion | bytes 2670592 | tf_op jit(solution)/shard_map/gather | solution.py:41
  103.8 1.7 copy.220
  105.6 1.6 reshape.456
  107.2 0.9 multiply_reduce_fusion
  108.0 1.3 reduce_sum.42
  109.5 3.8 %constant_dynamic-slice_fusion = (f32[3,512,1]{2,1,0:T(8,128)}, f32[3,512,1]{2,1,0:T(8,128)}, f32[3,512,1]{2,1,0:T(8,128)}, f32[3,512,1]{2,1,0:T(8,128)S(1)}, f3...) fusion(f32[3,512,8]{2,1,0:T(8,128)S(1)} %multiply_multiply_fusion, ...), kind=kLoop, calls=%fused_computation.99 | loop fusion | bytes 98336 | tf_op jit(solution)/shard_map/dynamic_slice | solution.py:115
  113.2 1.4 copy.233
  114.6 1.4 copy.231
  116.0 2.0 collective-permute-start
  118.0 1.5 collective-permute-start.1
  120.5 1.4 copy.243
  121.9 1.4 copy.241
  124.2 2.8 %collective-permute-start.3 = (f32[3,512,1]{1,2,0:T(1,128)S(1)}, f32[3,512,1]{1,2,0:T(1,128)}, u32[]{:S(2)}, u32[]{:S(2)}) collective-permute-start(f32[3,512,1]{1,2,0:T(1,128)S(1)} %copy.237), channel_id=1, source_target_pairs={{0,16},{4,20},{8,24},{12,28},{16,0},{20,4},{24,8},{28,12},{1,17},{... | collective-permute-start | bytes 18440 | tf_op jit(solution)/shard_map/ppermute | solution.py:117
  127.1 1.5 collective-permute-start.4
  128.5 3.3 %collective-permute-start.5 = (f32[3,512,1]{1,2,0:T(1,128)S(1)}, f32[3,512,1]{1,2,0:T(1,128)}, u32[]{:S(2)}, u32[]{:S(2)}) collective-permute-start(f32[3,512,1]{1,2,0:T(1,128)S(1)} %copy.241), channel_id=1, source_target_pairs={{0,24},{4,28},{8,16},{12,20},{16,8},{20,12},{24,0},{28,4},{1,25},{... | collective-permute-start | bytes 18440 | tf_op jit(solution)/shard_map/ppermute | solution.py:117
  133.1 3.1 %copy.230 = f32[3,512,1]{0,2,1:T(1,128)S(1)} copy(f32[3,512,1]{2,1,0:T(8,128)S(1)} %copy-done.4) | data formatting | bytes 12288 | tf_op jit(solution)/shard_map/dynamic_slice | solution.py:115
  136.3 5.9 %dynamic_update_slice.24 = f32[3,512,8]{0,2,1:T(8,128)S(1)} dynamic-update-slice(f32[3,512,8]{0,2,1:T(8,128)S(1)} %broadcast_in_dim.75, f32[3,512,1]{0,2,1:T(1,128)S(1)} %copy.230, s32[]{:T(128)} %constant.23.clone.1, s32[]{:T(128)} %constant.23.clone.1, s32[]{:T(128)S(6)} %select_n.82) | dynamic-update-slice | bytes 12292 | tf_op jit(solution)/shard_map/dynamic_update_slice | solution.py:118
  142.4 5.9 %dynamic_update_slice.25 = f32[3,512,8]{0,2,1:T(8,128)S(1)} dynamic-update-slice(f32[3,512,8]{0,2,1:T(8,128)S(1)} %dynamic_update_slice.24, f32[3,512,1]{0,2,1:T(1,128)S(1)} %copy.232, s32[]{:T(128)} %constant.23.clone.1, s32[]{:T(128)} %constant.23.clone.1, s32[]{:T(128)S(6)} %select_n.83) | dynamic-update-slice | bytes 12292 | tf_op jit(solution)/shard_map/dynamic_update_slice | solution.py:118
  148.5 5.9 %dynamic_update_slice.26 = f32[3,512,8]{0,2,1:T(8,128)S(1)} dynamic-update-slice(f32[3,512,8]{0,2,1:T(8,128)S(1)} %dynamic_update_slice.25, f32[3,512,1]{0,2,1:T(1,128)S(1)} %copy.234, s32[]{:T(128)} %constant.23.clone.1, s32[]{:T(128)} %constant.23.clone.1, s32[]{:T(128)S(6)} %select_n.84) | dynamic-update-slice | bytes 12292 | tf_op jit(solution)/shard_map/dynamic_update_slice | solution.py:118
  154.4 0.8 copy.236
  155.2 6.1 %dynamic_update_slice.27 = f32[3,512,8]{0,2,1:T(8,128)S(1)} dynamic-update-slice(f32[3,512,8]{0,2,1:T(8,128)S(1)} %dynamic_update_slice.26, f32[3,512,1]{0,2,1:T(1,128)S(1)} %copy.236, s32[]{:T(128)} %constant.23.clone.1, s32[]{:T(128)} %constant.23.clone.1, s32[]{:T(128)S(6)} %select_n.85) | dynamic-update-slice | bytes 12292 | tf_op jit(solution)/shard_map/dynamic_update_slice | solution.py:118
  162.2 5.9 %dynamic_update_slice.28 = f32[3,512,8]{0,2,1:T(8,128)S(1)} dynamic-update-slice(f32[3,512,8]{0,2,1:T(8,128)S(1)} %dynamic_update_slice.27, f32[3,512,1]{0,2,1:T(1,128)S(1)} %copy.238, s32[]{:T(128)} %constant.23.clone.1, s32[]{:T(128)} %constant.23.clone.1, s32[]{:T(128)S(6)} %select_n.86) | dynamic-update-slice | bytes 12292 | tf_op jit(solution)/shard_map/dynamic_update_slice | solution.py:118
  168.9 5.9 %dynamic_update_slice.29 = f32[3,512,8]{0,2,1:T(8,128)S(1)} dynamic-update-slice(f32[3,512,8]{0,2,1:T(8,128)S(1)} %dynamic_update_slice.28, f32[3,512,1]{0,2,1:T(1,128)S(1)} %copy.240, s32[]{:T(128)} %constant.23.clone.1, s32[]{:T(128)} %constant.23.clone.1, s32[]{:T(128)S(6)} %select_n.87) | dynamic-update-slice | bytes 12292 | tf_op jit(solution)/shard_map/dynamic_update_slice | solution.py:118
  175.7 5.9 %dynamic_update_slice.30 = f32[3,512,8]{0,2,1:T(8,128)S(1)} dynamic-update-slice(f32[3,512,8]{0,2,1:T(8,128)S(1)} %dynamic_update_slice.29, f32[3,512,1]{0,2,1:T(1,128)S(1)} %copy.242, s32[]{:T(128)} %constant.23.clone.1, s32[]{:T(128)} %constant.23.clone.1, s32[]{:T(128)S(6)} %select_n.88) | dynamic-update-slice | bytes 12292 | tf_op jit(solution)/shard_map/dynamic_update_slice | solution.py:118
  182.4 5.9 %dynamic_update_slice.31 = f32[3,512,8]{0,2,1:T(8,128)S(1)} dynamic-update-slice(f32[3,512,8]{0,2,1:T(8,128)S(1)} %dynamic_update_slice.30, f32[3,512,1]{0,2,1:T(1,128)S(1)} %copy.244, s32[]{:T(128)} %constant.23.clone.1, s32[]{:T(128)} %constant.23.clone.1, s32[]{:T(128)S(6)} %select_n.89) | dynamic-update-slice | bytes 12292 | tf_op jit(solution)/shard_map/dynamic_update_slice | solution.py:118
  188.3 7.6 %gather_fusion.3 = f32[2048,3]{1,0:T(8,128)} fusion(f32[4096,3]{1,0:T(8,128)S(1)} %bitcast.48, s32[2048]{0:T(1024)S(1)} %copy-done.19), kind=kCustom, calls=%fused_computation.3 | custom fusion | bytes 57344 | tf_op jit(solution)/shard_map/gather | solution.py:41
  195.9 1.6 copy.245
  198.6 12.4 %scatter_custom_fusion.4 = f32[1024,27]{1,0:T(8,128)} fusion(s32[2048]{0:T(1024)} %get-tuple-element.60, f32[2048,27]{1,0:T(8,128)S(1)} %copy.246, f32[]{:T(128)} %constant.22.clone.1), kind=kCustom, calls=%fused_computation.22 | custom fusion | flops 55296 | bytes 111104 | tf_op jit(solution)/shard_map/scatter-add | solution.py:46
  211.3 0.8 copy.225
  212.2 23.5 %scatter_custom_fusion.3 = f32[2048,81]{1,0:T(8,128)} fusion(s32[4096]{0:T(1024)} %bitcast.59, f32[4096,81]{1,0:T(8,128)S(1)} %copy.225, f32[]{:T(128)} %constant.22.clone.1), kind=kCustom, calls=%fused_computation.17 | custom fusion | flops 331776 | bytes 664064 | tf_op jit(solution)/shard_map/scatter-add | solution.py:46
  235.7 1.6 copy.248
  237.3 26.1 %reduce-scatter.3.cloned.1.call-done = f32[81,512]{0,1:T(8,128)} async-done(((f32[81,2048]{0,1:T(8,128)}), f32[81,512]{0,1:T(8,128)}) %reduce-scatter.3.cloned.1.call-update) | async-done | bytes 165904 | tf_op jit(solution)/shard_map/reduce_scatter | solution.py:134
  263.4 1.8 copy.247
  (146 shorter events, 19.7 us)
Async XLA Ops:
  7.2 8.2 %copy-start = (s32[2048,1]{0,1:T(1,128)S(1)}, s32[2048,1]{0,1:T(1,128)}, u32[]{:S(2)}) copy-start(s32[2048,1]{0,1:T(1,128)} %param.11) | copy-start | bytes 24580
  15.4 25.6 %copy-start.17 = (f32[3,2048]{1,0:T(4,128)S(1)}, f32[3,2048]{1,0:T(4,128)}, u32[]{:S(2)}) copy-start(f32[3,2048]{1,0:T(4,128)} %param.14) | copy-start | bytes 73732
  15.4 25.6 %copy-start.18 = (f32[3,2048]{1,0:T(4,128)S(1)}, f32[3,2048]{1,0:T(4,128)}, u32[]{:S(2)}) copy-start(f32[3,2048]{1,0:T(4,128)} %param.13) | copy-start | bytes 73732
  15.4 25.6 %copy-start.21 = (f32[2048]{0:T(1024)S(1)}, f32[2048]{0:T(1024)}, u32[]{:S(2)}) copy-start(f32[2048]{0:T(1024)} %param.15) | copy-start | bytes 24580
  58.3 10.6 %copy-start.15 = (s32[2048]{0:T(1024)S(1)}, s32[2048]{0:T(1024)}, u32[]{:S(2)}) copy-start(s32[2048]{0:T(1024)} %param.17) | copy-start | bytes 24580
  58.3 11.2 %copy-start.20 = (f32[2,2048]{1,0:T(2,128)S(1)}, f32[2,2048]{1,0:T(2,128)}, u32[]{:S(2)}) copy-start(f32[2,2048]{1,0:T(2,128)} %param.18) | copy-start | bytes 49156
  58.3 11.4 %copy-start.14 = (f32[27,256]{1,0:T(8,128)S(1)}, f32[27,256]{1,0:T(8,128)}, u32[]{:S(2)}) copy-start(f32[27,256]{1,0:T(8,128)} %param.19) | copy-start | bytes 82948
  61.5 23.2 %all-to-all-start = ((f32[8,512,8]{1,0,2:T(8,128)}), f32[8,512,8]{1,0,2:T(8,128)S(1)}, u32[]{:S(2)}, u32[]{:S(2)}) async-start(f32[8,512,8]{1,0,2:T(8,128)} %pad_maximum_fusion), calls=%async_computation | async-start | bytes 262144 | tf_op jit(solution)/shard_map/all_to_all | solution.py:102
  68.8 166.9 %reduce-scatter.5.cloned.1.call-start = ((), (), s32[]{:S(2)}) async-start(), calls=%async_computation.4 | async-start | bytes 655360 | tf_op jit(solution)/shard_map/reduce_scatter | solution.py:135
  82.5 1.1 copy-start.6
  82.9 1.2 copy-start.10
  84.1 4.7 %copy-start.8 = (f32[3,2048]{1,0:T(4,128)}, f32[3,2048]{1,0:T(4,128)S(1)}, u32[]{:S(2)}) copy-start(f32[3,2048]{1,0:T(4,128)S(1)} %multiply_reduce_fusion.1) | copy-start | bytes 73732
  86.8 1.7 copy-start.13
  105.6 1.6 copy-start.2
  107.1 2.2 copy-start.1
  107.2 2.2 copy-start.5
  109.5 10.0 %copy-start.16 = (f32[2048]{0:T(1024)S(1)}, f32[2048]{0:T(1024)}, u32[]{:S(2)}) copy-start(f32[2048]{0:T(1024)} %multiply_reduce_fusion.2) | copy-start | bytes 24580
  113.2 6.7 %copy-start.12 = (f32[1,512,8]{1,2,0:T(8,128)S(1)}, f32[1,512,8]{1,2,0:T(8,128)}, u32[]{:S(2)}) copy-start(f32[1,512,8]{1,2,0:T(8,128)} %get-tuple-element.48) | copy-start | bytes 49156
  116.0 12.5 %collective-permute-start = (f32[3,512,1]{1,2,0:T(1,128)S(1)}, f32[3,512,1]{1,2,0:T(1,128)S(1)}, u32[]{:S(2)}, u32[]{:S(2)}) collective-permute-start(f32[3,512,1]{1,2,0:T(1,128)S(1)} %copy.231), channel_id=1, source_target_pairs={{0,4},{4,0},{8,12},{12,8},{16,20},{20,16},{24,28},{28,24},{1,5},{5... | collective-permute-start | bytes 18440 | tf_op jit(solution)/shard_map/ppermute | solution.py:117
  118.0 13.8 %collective-permute-start.1 = (f32[3,512,1]{1,2,0:T(1,128)S(1)}, f32[3,512,1]{1,2,0:T(1,128)S(1)}, u32[]{:S(2)}, u32[]{:S(2)}) collective-permute-start(f32[3,512,1]{1,2,0:T(1,128)S(1)} %copy.233), channel_id=1, source_target_pairs={{0,8},{4,12},{8,0},{12,4},{16,24},{20,28},{24,16},{28,20},{1,9},{5... | collective-permute-start | bytes 18440 | tf_op jit(solution)/shard_map/ppermute | solution.py:117
  119.9 3.4 %copy-start.3 = (f32[3,512,1]{2,1,0:T(8,128)S(1)}, f32[3,512,1]{2,1,0:T(8,128)}, u32[]{:S(2)}) copy-start(f32[3,512,1]{2,1,0:T(8,128)} %get-tuple-element.30) | copy-start | bytes 18436
  120.3 12.7 %copy-start.7 = (f32[3,4096]{1,0:T(4,128)S(1)}, f32[3,4096]{1,0:T(4,128)}, u32[]{:S(2)}) copy-start(f32[3,4096]{1,0:T(4,128)} %multiply_reduce_fusion) | copy-start | bytes 147460
  123.6 9.5 %copy-start.4 = (f32[3,512,1]{2,1,0:T(8,128)S(1)}, f32[3,512,1]{2,1,0:T(8,128)}, u32[]{:S(2)}) copy-start(f32[3,512,1]{2,1,0:T(8,128)} %get-tuple-element.35) | copy-start | bytes 18436
  124.1 30.2 %collective-permute-start.2 = (f32[3,512,1]{1,2,0:T(1,128)S(1)}, f32[3,512,1]{1,2,0:T(1,128)}, u32[]{:S(2)}, u32[]{:S(2)}) collective-permute-start(f32[3,512,1]{1,2,0:T(1,128)S(1)} %copy.235), channel_id=1, source_target_pairs={{0,12},{4,8},{8,4},{12,0},{16,28},{20,24},{24,20},{28,16},{1,13},{... | collective-permute-start | bytes 18440 | tf_op jit(solution)/shard_map/ppermute | solution.py:117
  124.2 37.1 %collective-permute-start.3 = (f32[3,512,1]{1,2,0:T(1,128)S(1)}, f32[3,512,1]{1,2,0:T(1,128)}, u32[]{:S(2)}, u32[]{:S(2)}) collective-permute-start(f32[3,512,1]{1,2,0:T(1,128)S(1)} %copy.237), channel_id=1, source_target_pairs={{0,16},{4,20},{8,24},{12,28},{16,0},{20,4},{24,8},{28,12},{1,17},{... | collective-permute-start | bytes 18440 | tf_op jit(solution)/shard_map/ppermute | solution.py:117
  127.1 41.0 %collective-permute-start.4 = (f32[3,512,1]{1,2,0:T(1,128)S(1)}, f32[3,512,1]{1,2,0:T(1,128)}, u32[]{:S(2)}, u32[]{:S(2)}) collective-permute-start(f32[3,512,1]{1,2,0:T(1,128)S(1)} %copy.239), channel_id=1, source_target_pairs={{0,20},{4,16},{8,28},{12,24},{16,4},{20,0},{24,12},{28,8},{1,21},{... | collective-permute-start | bytes 18440 | tf_op jit(solution)/shard_map/ppermute | solution.py:117
  128.5 3.3 %copy-start.24 = (f32[3,512,1]{1,2,0:T(1,128)}, f32[3,512,1]{1,2,0:T(1,128)S(1)}, u32[]{:S(2)}) copy-start(f32[3,512,1]{1,2,0:T(1,128)S(1)} %collective-permute-done) | copy-start | bytes 18436
  128.5 46.3 %collective-permute-start.5 = (f32[3,512,1]{1,2,0:T(1,128)S(1)}, f32[3,512,1]{1,2,0:T(1,128)}, u32[]{:S(2)}, u32[]{:S(2)}) collective-permute-start(f32[3,512,1]{1,2,0:T(1,128)S(1)} %copy.241), channel_id=1, source_target_pairs={{0,24},{4,28},{8,16},{12,20},{16,8},{20,12},{24,0},{28,4},{1,25},{... | collective-permute-start | bytes 18440 | tf_op jit(solution)/shard_map/ppermute | solution.py:117
  131.8 0.6 copy-start.22
  132.4 49.1 %collective-permute-start.6 = (f32[3,512,1]{1,2,0:T(1,128)S(1)}, f32[3,512,1]{1,2,0:T(1,128)}, u32[]{:S(2)}, u32[]{:S(2)}) collective-permute-start(f32[3,512,1]{1,2,0:T(1,128)S(1)} %copy.243), channel_id=1, source_target_pairs={{0,28},{4,24},{8,20},{12,16},{16,12},{20,8},{24,4},{28,0},{1,29},{... | collective-permute-start | bytes 18440 | tf_op jit(solution)/shard_map/ppermute | solution.py:117
  133.0 9.2 %copy-start.25 = (f32[3,512,1]{1,2,0:T(1,128)S(1)}, f32[3,512,1]{1,2,0:T(1,128)}, u32[]{:S(2)}) copy-start(f32[3,512,1]{1,2,0:T(1,128)} %copy-done.24) | copy-start | bytes 18436
  133.1 15.2 %copy-start.23 = (f32[3,512,1]{1,2,0:T(1,128)S(1)}, f32[3,512,1]{1,2,0:T(1,128)}, u32[]{:S(2)}) copy-start(f32[3,512,1]{1,2,0:T(1,128)} %copy-done.22) | copy-start | bytes 18436
  154.3 33.9 %copy-start.19 = (s32[2048]{0:T(1024)S(1)}, s32[2048]{0:T(1024)}, u32[]{:S(2)}) copy-start(s32[2048]{0:T(1024)} %get-tuple-element.62) | copy-start | bytes 24580
  188.3 9.2 %copy-start.9 = (f32[3,2048]{1,0:T(4,128)S(1)}, f32[3,2048]{1,0:T(4,128)}, u32[]{:S(2)}) copy-start(f32[3,2048]{1,0:T(4,128)} %copy-done.8) | copy-start | bytes 73732
  188.3 9.2 %copy-start.11 = (f32[3,2048]{1,0:T(4,128)S(1)}, f32[3,2048]{1,0:T(4,128)}, u32[]{:S(2)}) copy-start(f32[3,2048]{1,0:T(4,128)} %param.16) | copy-start | bytes 73732
  211.0 52.4 %reduce-scatter.3.cloned.1.call-start = ((), (), s32[]{:S(2)}) async-start(), calls=%async_computation.3 | async-start | bytes 1310720 | tf_op jit(solution)/shard_map/reduce_scatter | solution.py:134
Sparse Core Ops, SparseCore 0:
  211.1 21.8 reduce-scatter.4
  235.8 27.5 reduce-scatter.2
